TPU v7x, 256 devices: a whole 4x4x8 slice. The times are simulated.
256 devices in a mesh: grp: 4 (over z_hi), freq: 64 (over z_lo, y, x, core).
Axes of the slice: x: 4, y: 4, z: 8 (z_hi: 4, z_lo: 2; z = z_hi * 2 + z_lo), core: 2. Of those that a mesh axis runs over, the one named last changes fastest.
Arguments:
- sources: bfloat16 [1024, 262144], P('freq', 'grp'), may hold values from -6 to 6
- panel_pos: float32 [3, 262144], P(None, 'grp'), may hold values from -1 to 1
- panel_blade: int32 [262144], P('grp'), may hold values from 0 to 3
- observer_table: float32 [3, 2048], replicated, may hold values from -8 to 8, as said below
- observer_index: int32 [32], replicated, may hold values from 0 to 2047
Outputs:
- spectra: float32 [512, 4, 2, 32], P('freq', 'grp')
Inputs may be any that keep to these rules, and one draw needn't show every extreme that they name: `observer_table`: each observer lies 3 to 8 units from the anchor (0, 0, 0).
All inputs are finite; a program needn't handle non-finite values.
Results may differ from a plain program's by a relative error of at most 0.0047.
Values may be sent and summed in bfloat16 or wider, within the bound.
No kernel may reach another device: no remote copies, remote signals or barrier semaphores. Data moves between devices by JAX's collectives and lax.ppermute only.
A program may use at most 64 MiB of HBM per device.

v0:
```python
import math
import jax
import jax.numpy as jnp
from jax import lax
from jax.sharding import PartitionSpec as P

NT = 1024
NF = 512
NCOMP = 4
wave_step = 0.04


def over_pieces(x, axis):
    return lax.all_gather(x, axis).sum(0)


def transform_table():
    row_index = jnp.arange(2 * NF, dtype=jnp.int32)
    samples = jnp.arange(NT, dtype=jnp.int32)
    frequency = row_index // 2
    parity = row_index % 2
    turn_count = frequency[:, None] * samples[None, :] % NT
    angle_table = 2.0 * math.pi / NT * turn_count.astype(jnp.float32)
    values = jnp.where(parity[:, None] == 0, jnp.cos(angle_table), -jnp.sin(angle_table))
    return (values / math.sqrt(NT)).astype(jnp.bfloat16)


def distances(positions, observers):
    offset_x = observers[0][:, None] - positions[0][None, :]
    offset_y = observers[1][:, None] - positions[1][None, :]
    offset_z = observers[2][:, None] - positions[2][None, :]
    return jnp.sqrt(offset_x * offset_x + offset_y * offset_y + offset_z * offset_z)


def blade_masks(blades):
    return (blades[None, :] == jnp.arange(NCOMP, dtype=jnp.int32)[:, None]).astype(jnp.bfloat16)


def frequency_term(frequency, spectrum_pair, blade_mask, distance, amplitude):
    wavenumber = wave_step * frequency.astype(jnp.float32)
    phase_angle = wavenumber * distance
    green_matrix = jnp.concatenate(
        [jnp.cos(phase_angle) * amplitude, -jnp.sin(phase_angle) * amplitude], axis=0
    ).astype(jnp.bfloat16)
    weighted = jnp.concatenate(
        [spectrum_pair[0][None, :] * blade_mask, spectrum_pair[1][None, :] * blade_mask], axis=0
    )
    product = lax.dot_general(
        weighted, green_matrix, (((1,), (1,)), ((), ())), preferred_element_type=jnp.float32
    )
    blade_count = blade_mask.shape[0]
    observer_count = distance.shape[0]
    real_part = product[:blade_count, :observer_count] - product[blade_count:, observer_count:]
    imag_part = product[:blade_count, observer_count:] + product[blade_count:, :observer_count]
    return jnp.stack([real_part, imag_part], axis=1)


def body(sources, panel_pos, panel_blade, observer_table, observer_index):
    freq_share = NF // lax.axis_size("freq")
    position = lax.axis_index("freq")
    observers = observer_table[:, observer_index]
    dft_table = transform_table()
    exchanged = lax.all_to_all(sources, "freq", split_axis=1, concat_axis=0, tiled=True)
    spectrum = jnp.dot(dft_table, exchanged, preferred_element_type=jnp.float32).astype(
        jnp.bfloat16
    )
    received = lax.all_to_all(spectrum, "freq", split_axis=0, concat_axis=1, tiled=True)
    spectra_pairs = received.reshape(freq_share, 2, received.shape[1])
    distance = distances(panel_pos, observers)
    amplitude = 0.25 / (math.pi * distance)
    blade_mask = blade_masks(panel_blade)
    frequencies = position * freq_share + jnp.arange(freq_share, dtype=jnp.int32)

    def per_frequency(element):
        return frequency_term(element[0], element[1], blade_mask, distance, amplitude)

    partial_value = lax.map(per_frequency, (frequencies, spectra_pairs))
    summed = over_pieces(partial_value, "grp")
    blade_share = NCOMP // lax.axis_size("grp")
    return lax.dynamic_slice_in_dim(summed, lax.axis_index("grp") * blade_share, blade_share, 1)


def solution(mesh):
    in_specs = (P("freq", "grp"), P(None, "grp"), P("grp"), P(), P())
    out_specs = P("freq", "grp", None, None)
    return jax.shard_map(body, mesh=mesh, in_specs=in_specs, out_specs=out_specs, check_vma=False)
```

profile of v0, /device:TPU:2, one launch (start us, length us, event | category | flops | bytes accessed | tf_op | source)
XLA Modules:
  0.0 451.5 jit_solution(7879830638706427243)
XLA Ops:
  0.0 3.2 copy.19
  3.2 9.4 %all-to-all-start = ((bf16[16,64,1024]{2,0,1:T(8,128)(2,1)}), bf16[16,64,1024]{2,0,1:T(8,128)(2,1)S(1)}, u32[]{:S(2)}, u32[]{:S(2)}) async-start(bf16[16,64,1024]{2,0,1:T(8,128)(2,1)} %bitcast.24), calls=%async_computation | async-start | bytes 4194304 | tf_op jit(solution)/shard_map/all_to_all | solution.py:63
  12.6 27.8 %all-to-all-done = bf16[16,64,1024]{2,0,1:T(8,128)(2,1)S(1)} async-done(((bf16[16,64,1024]{2,0,1:T(8,128)(2,1)}), bf16[16,64,1024]{2,0,1:T(8,128)(2,1)S(1)}, u32[]{:S(2)}, u32[]{:S(2)}) %all-to-all-start) | async-done | bytes 2097184 | tf_op jit(solution)/shard_map/all_to_all | solution.py:63
  40.4 21.4 %fusion.32 = bf16[1024,1024]{1,0:T(8,128)(2,1)} fusion(bf16[1024,1024]{1,0:T(8,128)(2,1)S(1)} %bitcast.34, s32[1024]{0:T(1024)S(1)} %add_select_fusion.1, pred[1024]{0:T(1024)(128)(4,1)S(1)} %fusion.33), kind=kOutput, calls=%fused_computation.45 | convolution fusion | flops 2167406592 | bytes 4199424 | tf_op jit(solution)/shard_map/dot_general | solution.py:64
  61.8 7.3 %all-to-all-start.1 = ((bf16[64,16,1024]{2,1,0:T(8,128)(2,1)}), bf16[64,16,1024]{2,1,0:T(8,128)(2,1)S(1)}, u32[]{:S(2)}, u32[]{:S(2)}) async-start(bf16[64,16,1024]{2,1,0:T(8,128)(2,1)} %bitcast.33), calls=%async_computation.1 | async-start | bytes 4194304 | tf_op jit(solution)/shard_map/all_to_all | solution.py:67
  69.1 0.0 copy-done.1
  69.1 1.4 fusion.44
  70.6 0.4 copy.15
  71.0 0.6 gather_fusion
  71.6 0.2 slice_reduce_fusion
  71.8 25.2 %all-to-all-done.1 = bf16[64,16,1024]{2,1,0:T(8,128)(2,1)S(1)} async-done(((bf16[64,16,1024]{2,1,0:T(8,128)(2,1)}), bf16[64,16,1024]{2,1,0:T(8,128)(2,1)S(1)}, u32[]{:S(2)}, u32[]{:S(2)}) %all-to-all-start.1) | async-done | bytes 2097184 | tf_op jit(solution)/shard_map/all_to_all | solution.py:67
  97.0 2.5 copy.14
  99.5 4.9 %reshape.45 = bf16[8,2,65536]{2,1,0:T(2,128)(2,1)S(1)} reshape(bf16[16,64,1024]{2,1,0:T(8,128)(2,1)} %copy.14) | data formatting | bytes 4194304 | tf_op jit(solution)/shard_map/reshape | solution.py:68
  104.4 329.8 %while.12 = (s32[]{:T(128)}, f32[8,4,2,32]{3,1,2,0:T(4,128)S(1)}, bf16[8,2,65536]{2,1,0:T(2,128)(2,1)S(1)}, s32[8]{0:T(128)S(1)}, s32[65536]{0:T(1024)S(1)}, /*i...) while((s32[]{:T(128)}, f32[8,4,2,32]{3,1,2,0:T(4,128)S(1)}, ...), condition=%wide.region_1.2_spmd.clone.clone, body=%wide.region_0.1_spmd.clone.clone.sunk | while | flops 120324608 | bytes 20723280 | solution.py:77
  104.4 0.6 dynamic_slice.18
  105.6 1.4 dynamic-slice_reduce_fusion.3
  107.0 0.5 fusion.53
  107.5 35.8 %multiply_convert_fusion.7 = (bf16[32,65536]{1,0:T(8,128)(2,1)S(1)}, bf16[32,65536]{1,0:T(8,128)(2,1)S(1)}) fusion(f32[65536]{0:T(1024)S(1)} %get-tuple-element.290, f32[32]{0:T(128)S(1)} %get-tuple-element.291, f32[65536]{0:T(1024)S(1)} %get-tuple-element.288, f32[32]{0:T(128)S(1)} %get-tuple-element.289, f32[65536]{0:T(1024)S(1)} %get-tuple-element.286, ...), kind=kLoop, calls=%fused_computation.11.clone.1 | loop fusion | flops 33554432 | bytes 9175428 | tf_op jit(solution)/shard_map/convert
  143.3 2.3 fusion.54
  145.5 0.1 subtract_bitcast_fusion.2
  145.6 0.6 dynamic_slice.18
  146.8 1.4 dynamic-slice_reduce_fusion.3
  148.2 0.5 fusion.53
  148.7 35.8 %multiply_convert_fusion.7 = (bf16[32,65536]{1,0:T(8,128)(2,1)S(1)}, bf16[32,65536]{1,0:T(8,128)(2,1)S(1)}) fusion(f32[65536]{0:T(1024)S(1)} %get-tuple-element.290, f32[32]{0:T(128)S(1)} %get-tuple-element.291, f32[65536]{0:T(1024)S(1)} %get-tuple-element.288, f32[32]{0:T(128)S(1)} %get-tuple-element.289, f32[65536]{0:T(1024)S(1)} %get-tuple-element.286, ...), kind=kLoop, calls=%fused_computation.11.clone.1 | loop fusion | flops 33554432 | bytes 9175428 | tf_op jit(solution)/shard_map/convert
  184.5 2.3 fusion.54
  186.8 0.1 subtract_bitcast_fusion.2
  186.9 0.6 dynamic_slice.18
  188.0 1.4 dynamic-slice_reduce_fusion.3
  189.4 0.5 fusion.53
  189.9 35.8 %multiply_convert_fusion.7 = (bf16[32,65536]{1,0:T(8,128)(2,1)S(1)}, bf16[32,65536]{1,0:T(8,128)(2,1)S(1)}) fusion(f32[65536]{0:T(1024)S(1)} %get-tuple-element.290, f32[32]{0:T(128)S(1)} %get-tuple-element.291, f32[65536]{0:T(1024)S(1)} %get-tuple-element.288, f32[32]{0:T(128)S(1)} %get-tuple-element.289, f32[65536]{0:T(1024)S(1)} %get-tuple-element.286, ...), kind=kLoop, calls=%fused_computation.11.clone.1 | loop fusion | flops 33554432 | bytes 9175428 | tf_op jit(solution)/shard_map/convert
  225.7 2.3 fusion.54
  228.0 0.1 subtract_bitcast_fusion.2
  228.1 0.6 dynamic_slice.18
  229.2 1.4 dynamic-slice_reduce_fusion.3
  230.7 0.5 fusion.53
  231.1 35.8 %multiply_convert_fusion.7 = (bf16[32,65536]{1,0:T(8,128)(2,1)S(1)}, bf16[32,65536]{1,0:T(8,128)(2,1)S(1)}) fusion(f32[65536]{0:T(1024)S(1)} %get-tuple-element.290, f32[32]{0:T(128)S(1)} %get-tuple-element.291, f32[65536]{0:T(1024)S(1)} %get-tuple-element.288, f32[32]{0:T(128)S(1)} %get-tuple-element.289, f32[65536]{0:T(1024)S(1)} %get-tuple-element.286, ...), kind=kLoop, calls=%fused_computation.11.clone.1 | loop fusion | flops 33554432 | bytes 9175428 | tf_op jit(solution)/shard_map/convert
  266.9 2.3 fusion.54
  269.2 0.1 subtract_bitcast_fusion.2
  269.3 0.6 dynamic_slice.18
  270.5 1.4 dynamic-slice_reduce_fusion.3
  271.9 0.5 fusion.53
  272.4 35.8 %multiply_convert_fusion.7 = (bf16[32,65536]{1,0:T(8,128)(2,1)S(1)}, bf16[32,65536]{1,0:T(8,128)(2,1)S(1)}) fusion(f32[65536]{0:T(1024)S(1)} %get-tuple-element.290, f32[32]{0:T(128)S(1)} %get-tuple-element.291, f32[65536]{0:T(1024)S(1)} %get-tuple-element.288, f32[32]{0:T(128)S(1)} %get-tuple-element.289, f32[65536]{0:T(1024)S(1)} %get-tuple-element.286, ...), kind=kLoop, calls=%fused_computation.11.clone.1 | loop fusion | flops 33554432 | bytes 9175428 | tf_op jit(solution)/shard_map/convert
  308.2 2.3 fusion.54
  310.4 0.1 subtract_bitcast_fusion.2
  310.5 0.6 dynamic_slice.18
  311.7 1.4 dynamic-slice_reduce_fusion.3
  313.1 0.5 fusion.53
  313.6 35.8 %multiply_convert_fusion.7 = (bf16[32,65536]{1,0:T(8,128)(2,1)S(1)}, bf16[32,65536]{1,0:T(8,128)(2,1)S(1)}) fusion(f32[65536]{0:T(1024)S(1)} %get-tuple-element.290, f32[32]{0:T(128)S(1)} %get-tuple-element.291, f32[65536]{0:T(1024)S(1)} %get-tuple-element.288, f32[32]{0:T(128)S(1)} %get-tuple-element.289, f32[65536]{0:T(1024)S(1)} %get-tuple-element.286, ...), kind=kLoop, calls=%fused_computation.11.clone.1 | loop fusion | flops 33554432 | bytes 9175428 | tf_op jit(solution)/shard_map/convert
  349.4 2.3 fusion.54
  351.7 0.1 subtract_bitcast_fusion.2
  351.7 0.6 dynamic_slice.18
  352.9 1.4 dynamic-slice_reduce_fusion.3
  354.3 0.5 fusion.53
  354.8 35.8 %multiply_convert_fusion.7 = (bf16[32,65536]{1,0:T(8,128)(2,1)S(1)}, bf16[32,65536]{1,0:T(8,128)(2,1)S(1)}) fusion(f32[65536]{0:T(1024)S(1)} %get-tuple-element.290, f32[32]{0:T(128)S(1)} %get-tuple-element.291, f32[65536]{0:T(1024)S(1)} %get-tuple-element.288, f32[32]{0:T(128)S(1)} %get-tuple-element.289, f32[65536]{0:T(1024)S(1)} %get-tuple-element.286, ...), kind=kLoop, calls=%fused_computation.11.clone.1 | loop fusion | flops 33554432 | bytes 9175428 | tf_op jit(solution)/shard_map/convert
  390.6 2.3 fusion.54
  392.9 0.1 subtract_bitcast_fusion.2
  393.0 0.6 dynamic_slice.18
  394.1 1.4 dynamic-slice_reduce_fusion.3
  395.5 0.5 fusion.53
  396.0 35.8 %multiply_convert_fusion.7 = (bf16[32,65536]{1,0:T(8,128)(2,1)S(1)}, bf16[32,65536]{1,0:T(8,128)(2,1)S(1)}) fusion(f32[65536]{0:T(1024)S(1)} %get-tuple-element.290, f32[32]{0:T(128)S(1)} %get-tuple-element.291, f32[65536]{0:T(1024)S(1)} %get-tuple-element.288, f32[32]{0:T(128)S(1)} %get-tuple-element.289, f32[65536]{0:T(1024)S(1)} %get-tuple-element.286, ...), kind=kLoop, calls=%fused_computation.11.clone.1 | loop fusion | flops 33554432 | bytes 9175428 | tf_op jit(solution)/shard_map/convert
  431.8 2.3 fusion.54
  434.1 0.1 subtract_bitcast_fusion.2
  434.2 16.6 %all-gather = f32[32,4,2,32]{3,1,2,0:T(4,128)S(1)} all-gather(f32[8,4,2,32]{3,1,2,0:T(4,128)S(1)} %get-tuple-element.42), channel_id=2, replica_groups=mesh['grp'=4,'freq'=64] {'grp'}, dimensions={0}, use_global_device_ids=true | all-gather | bytes 40960 | tf_op jit(solution)/shard_map/all_gather | solution.py:14
  450.8 0.6 constant_dynamic-slice_fusion
  (28 shorter events, 0.2 us)
Async XLA Ops:
  3.2 37.2 %all-to-all-start = ((bf16[16,64,1024]{2,0,1:T(8,128)(2,1)}), bf16[16,64,1024]{2,0,1:T(8,128)(2,1)S(1)}, u32[]{:S(2)}, u32[]{:S(2)}) async-start(bf16[16,64,1024]{2,0,1:T(8,128)(2,1)} %bitcast.24), calls=%async_computation | async-start | bytes 4194304 | tf_op jit(solution)/shard_map/all_to_all | solution.py:63
  61.8 7.3 %copy-start.1 = (f32[3,65536]{1,0:T(4,128)S(1)}, f32[3,65536]{1,0:T(4,128)}, u32[]{:S(2)}) copy-start(f32[3,65536]{1,0:T(4,128)} %param.8) | copy-start | bytes 2359300
  61.8 8.8 %copy-start.5 = (f32[3,2048]{1,0:T(4,128)S(1)}, f32[3,2048]{1,0:T(4,128)}, u32[]{:S(2)}) copy-start(f32[3,2048]{1,0:T(4,128)} %param.10) | copy-start | bytes 73732
  61.8 9.2 %copy-start.6 = (s32[32]{0:T(128)S(1)}, s32[32]{0:T(128)}, u32[]{:S(2)}) copy-start(s32[32]{0:T(128)} %param.11) | copy-start | bytes 388
  61.8 35.2 %all-to-all-start.1 = ((bf16[64,16,1024]{2,1,0:T(8,128)(2,1)}), bf16[64,16,1024]{2,1,0:T(8,128)(2,1)S(1)}, u32[]{:S(2)}, u32[]{:S(2)}) async-start(bf16[64,16,1024]{2,1,0:T(8,128)(2,1)} %bitcast.33), calls=%async_computation.1 | async-start | bytes 4194304 | tf_op jit(solution)/shard_map/all_to_all | solution.py:67
  97.0 7.4 %copy-start = (s32[65536]{0:T(1024)S(1)}, s32[65536]{0:T(1024)}, u32[]{:S(2)}) copy-start(s32[65536]{0:T(1024)} %param.9) | copy-start | bytes 786436
  97.0 7.4 %copy-start.2 = (f32[1,65536]{1,0:T(1,128)S(1)}, f32[1,65536]{1,0:T(1,128)}, u32[]{:S(2)}) copy-start(f32[1,65536]{1,0:T(1,128)} %get-tuple-element.165) | copy-start | bytes 786436
  97.0 7.4 %copy-start.3 = (f32[1,65536]{1,0:T(1,128)S(1)}, f32[1,65536]{1,0:T(1,128)}, u32[]{:S(2)}) copy-start(f32[1,65536]{1,0:T(1,128)} %get-tuple-element.166) | copy-start | bytes 786436
  97.0 7.4 %copy-start.4 = (f32[1,65536]{1,0:T(1,128)S(1)}, f32[1,65536]{1,0:T(1,128)}, u32[]{:S(2)}) copy-start(f32[1,65536]{1,0:T(1,128)} %get-tuple-element.167) | copy-start | bytes 786436
where the time goes:
time: 452 us; the launch traced here: 451 us
  other arithmetic  291 us (64%)
  waiting for transfers between devices  53 us (12%)
  matrix products  39.5 us (9%)
  local copies, waits for them, and re-layouts  29.8 us (7%)
  starting transfers between devices  16.7 us (4%)
  blocking collectives  16.6 us (4%)
  loops' own time  4.72 us (1%)
    another operation x8, other arithmetic  286 us
    all_to_all x1, waiting for transfers between devices, body(): lax.all_to_all(sources, 'freq', split_axis=1, concat_axis=0, tiled=True)  27.8 us
    all_to_all x1, waiting for transfers between devices, body(): lax.all_to_all(spectrum, 'freq', split_axis=0, concat_axis=1, tiled=True)  25.2 us
    dot_general x1, matrix products, body(): jnp.dot(dft_table, exchanged, preferred_element_type=jnp.float32)  21.4 us
    dot_general x8, matrix products, frequency_term(): lax.dot_general(weighted, green_matrix, (((1,), (1,)), ((), ())), preferr...  18.1 us
    all_gather x1, blocking collectives, over_pieces(): return lax.all_gather(x, axis).sum(0)  16.6 us
    slice x8, local copies, waits for them, and re-layouts, frequency_term(): spectrum_pair[0][None, :] * blade_mask  11.3 us
    all_to_all x1, starting transfers between devices, body(): lax.all_to_all(sources, 'freq', split_axis=1, concat_axis=0, tiled=True)  9.37 us
  transfers between devices with their start and end apart: 2, of which 2 were waited for; matrix products, arithmetic and copies ran while one was open for 1% of the time, Pallas kernels for 0%

commit v1 on v0

--- a/solution.py
+++ b/solution.py
@@ -60,7 +60,10 @@
     position = lax.axis_index("freq")
     observers = observer_table[:, observer_index]
     dft_table = transform_table()
-    exchanged = lax.all_to_all(sources, "freq", split_axis=1, concat_axis=0, tiled=True)
+    count = lax.axis_size("freq")
+    blocks = jnp.stack(jnp.split(sources, count, axis=1), axis=0)
+    blocks = lax.all_to_all(blocks, "freq", split_axis=0, concat_axis=0)
+    exchanged = jnp.concatenate(blocks, axis=0)
     spectrum = jnp.dot(dft_table, exchanged, preferred_element_type=jnp.float32).astype(
         jnp.bfloat16
     )

time: 452 us -> 542 us (1.20)
  local copies, waits for them, and re-layouts: 29.8 us -> 114 us
    unnamed x15 -> x76, local copies, waits for them, and re-layouts: 0.38 us -> 86.1 us
  transfers between devices with their start and end apart: 2 -> 2, of which waited for: 2 -> 2; matrix products, arithmetic and copies ran while one was open for 1% -> 0% of each run, Pallas kernels for 0% -> 0%
where the time goes in v1:
time: 542 us; the launch traced here: 537 us
  other arithmetic  291 us (54%)
  local copies, waits for them, and re-layouts  114 us (21%)
  waiting for transfers between devices  53.1 us (10%)
  matrix products  39.5 us (7%)
  starting transfers between devices  16.7 us (3%)
  blocking collectives  16.6 us (3%)
  loops' own time  5.76 us (1%)
    another operation x8, other arithmetic  286 us
    unnamed x76, local copies, waits for them, and re-layouts  86.1 us
    all_to_all x1, waiting for transfers between devices, body(): blocks = lax.all_to_all(blocks, 'freq', split_axis=0, concat_axis=0)  27.8 us
    all_to_all x1, waiting for transfers between devices, body(): lax.all_to_all(spectrum, 'freq', split_axis=0, concat_axis=1, tiled=True)  25.3 us
    dot_general x1, matrix products, body(): jnp.dot(dft_table, exchanged, preferred_element_type=jnp.float32)  21.4 us
    dot_general x8, matrix products, frequency_term(): lax.dot_general(weighted, green_matrix, (((1,), (1,)), ((), ())), preferr...  18.1 us
    all_gather x1, blocking collectives, over_pieces(): return lax.all_gather(x, axis).sum(0)  16.6 us
    slice x8, local copies, waits for them, and re-layouts, frequency_term(): spectrum_pair[0][None, :] * blade_mask  11.3 us
  transfers between devices with their start and end apart: 2, of which 2 were waited for; matrix products, arithmetic and copies ran while one was open for 0% of the time, Pallas kernels for 0%

profile of v1, /device:TPU:2, one launch (start us, length us, event | category | flops | bytes accessed | tf_op | source)
XLA Modules:
  0.0 537.2 jit_solution(17654106578965600208)
XLA Ops:
  1.4 1.4 constant_dynamic-update-slice_fusion.62
  4.1 1.4 constant_dynamic-update-slice_fusion.60
  6.8 1.4 constant_dynamic-update-slice_fusion.58
  9.5 1.4 constant_dynamic-update-slice_fusion.56
  12.3 1.4 constant_dynamic-update-slice_fusion.54
  13.6 1.4 constant_dynamic-update-slice_fusion.53
  15.0 1.4 constant_dynamic-update-slice_fusion.52
  17.7 1.4 constant_dynamic-update-slice_fusion.50
  19.1 1.4 constant_dynamic-update-slice_fusion.49
  21.8 1.4 constant_dynamic-update-slice_fusion.47
  23.2 1.4 constant_dynamic-update-slice_fusion.46
  25.9 1.4 constant_dynamic-update-slice_fusion.44
  28.6 1.4 constant_dynamic-update-slice_fusion.42
  36.8 1.4 constant_dynamic-update-slice_fusion.36
  38.1 1.4 constant_dynamic-update-slice_fusion.35
  40.8 1.4 constant_dynamic-update-slice_fusion.33
  42.2 1.4 constant_dynamic-update-slice_fusion.32
  44.9 1.4 constant_dynamic-update-slice_fusion.30
  46.3 1.4 constant_dynamic-update-slice_fusion.29
  47.7 1.4 constant_dynamic-update-slice_fusion.28
  50.4 1.4 constant_dynamic-update-slice_fusion.26
  53.1 1.4 constant_dynamic-update-slice_fusion.24
  58.6 1.4 constant_dynamic-update-slice_fusion.20
  61.3 1.4 constant_dynamic-update-slice_fusion.18
  64.0 1.4 constant_dynamic-update-slice_fusion.16
  69.5 1.4 constant_dynamic-update-slice_fusion.12
  72.2 1.4 constant_dynamic-update-slice_fusion.10
  74.9 1.4 constant_dynamic-update-slice_fusion.8
  80.4 1.4 constant_dynamic-update-slice_fusion.4
  81.7 1.4 constant_dynamic-update-slice_fusion.3
  85.8 1.4 constant_dynamic-update-slice_fusion
  87.2 9.4 %all-to-all-start = ((bf16[64,16,1024]{2,1,0:T(8,128)(2,1)}), bf16[64,16,1024]{2,1,0:T(8,128)(2,1)S(1)}, u32[]{:S(2)}, u32[]{:S(2)}) async-start(bf16[64,16,1024]{2,1,0:T(8,128)(2,1)} %constant_dynamic-update-slice_fusion), calls=%async_computation | async-start | bytes 4194304 | tf_op jit(solution)/shard_map/all_to_all | solution.py:65
  96.6 27.8 %all-to-all-done = bf16[64,16,1024]{2,1,0:T(8,128)(2,1)S(1)} async-done(((bf16[64,16,1024]{2,1,0:T(8,128)(2,1)}), bf16[64,16,1024]{2,1,0:T(8,128)(2,1)S(1)}, u32[]{:S(2)}, u32[]{:S(2)}) %all-to-all-start) | async-done | bytes 2097184 | tf_op jit(solution)/shard_map/all_to_all | solution.py:65
  124.4 21.4 %fusion.32 = bf16[1024,1024]{1,0:T(8,128)(2,1)} fusion(bf16[1024,1024]{1,0:T(8,128)(2,1)S(1)} %bitcast.155, s32[1024]{0:T(1024)S(1)} %add_select_fusion.1, pred[1024]{0:T(1024)(128)(4,1)S(1)} %fusion.33), kind=kOutput, calls=%fused_computation.44 | convolution fusion | flops 2167406592 | bytes 4199424 | tf_op jit(solution)/shard_map/dot_general | solution.py:67
  145.8 7.3 %all-to-all-start.1 = ((bf16[64,16,1024]{2,1,0:T(8,128)(2,1)}), bf16[64,16,1024]{2,1,0:T(8,128)(2,1)S(1)}, u32[]{:S(2)}, u32[]{:S(2)}) async-start(bf16[64,16,1024]{2,1,0:T(8,128)(2,1)} %bitcast.154), calls=%async_computation.1 | async-start | bytes 4194304 | tf_op jit(solution)/shard_map/all_to_all | solution.py:70
  155.7 25.3 %all-to-all-done.1 = bf16[64,16,1024]{2,1,0:T(8,128)(2,1)S(1)} async-done(((bf16[64,16,1024]{2,1,0:T(8,128)(2,1)}), bf16[64,16,1024]{2,1,0:T(8,128)(2,1)S(1)}, u32[]{:S(2)}, u32[]{:S(2)}) %all-to-all-start.1) | async-done | bytes 2097184 | tf_op jit(solution)/shard_map/all_to_all | solution.py:70
  181.0 2.5 copy.10
  183.5 5.0 reshape.46
  188.5 331.5 %while.12 = (s32[]{:T(128)}, f32[8,4,2,32]{3,1,2,0:T(4,128)S(1)}, bf16[8,2,65536]{2,1,0:T(2,128)(2,1)S(1)}, s32[8]{0:T(128)S(1)}, s32[65536]{0:T(1024)S(1)}, /*i...) while((s32[]{:T(128)}, f32[8,4,2,32]{3,1,2,0:T(4,128)S(1)}, ...), condition=%wide.region_1.2_spmd.clone.clone, body=%wide.region_0.1_spmd.clone.clone.sunk | while | flops 120324608 | bytes 20723280 | solution.py:80
  189.8 1.4 dynamic-slice_reduce_fusion.3
  191.7 35.8 %multiply_convert_fusion.7 = (bf16[32,65536]{1,0:T(8,128)(2,1)S(1)}, bf16[32,65536]{1,0:T(8,128)(2,1)S(1)}) fusion(f32[65536]{0:T(1024)S(1)} %get-tuple-element.290, f32[32]{0:T(128)S(1)} %get-tuple-element.291, f32[65536]{0:T(1024)S(1)} %get-tuple-element.288, f32[32]{0:T(128)S(1)} %get-tuple-element.289, f32[65536]{0:T(1024)S(1)} %get-tuple-element.286, ...), kind=kLoop, calls=%fused_computation.11.clone.1 | loop fusion | flops 33554432 | bytes 9175428 | tf_op jit(solution)/shard_map/convert
  227.5 2.3 fusion.54
  231.3 1.4 dynamic-slice_reduce_fusion.3
  233.2 35.8 %multiply_convert_fusion.7 = (bf16[32,65536]{1,0:T(8,128)(2,1)S(1)}, bf16[32,65536]{1,0:T(8,128)(2,1)S(1)}) fusion(f32[65536]{0:T(1024)S(1)} %get-tuple-element.290, f32[32]{0:T(128)S(1)} %get-tuple-element.291, f32[65536]{0:T(1024)S(1)} %get-tuple-element.288, f32[32]{0:T(128)S(1)} %get-tuple-element.289, f32[65536]{0:T(1024)S(1)} %get-tuple-element.286, ...), kind=kLoop, calls=%fused_computation.11.clone.1 | loop fusion | flops 33554432 | bytes 9175428 | tf_op jit(solution)/shard_map/convert
  269.0 2.3 fusion.54
  272.7 1.4 dynamic-slice_reduce_fusion.3
  274.6 35.8 %multiply_convert_fusion.7 = (bf16[32,65536]{1,0:T(8,128)(2,1)S(1)}, bf16[32,65536]{1,0:T(8,128)(2,1)S(1)}) fusion(f32[65536]{0:T(1024)S(1)} %get-tuple-element.290, f32[32]{0:T(128)S(1)} %get-tuple-element.291, f32[65536]{0:T(1024)S(1)} %get-tuple-element.288, f32[32]{0:T(128)S(1)} %get-tuple-element.289, f32[65536]{0:T(1024)S(1)} %get-tuple-element.286, ...), kind=kLoop, calls=%fused_computation.11.clone.1 | loop fusion | flops 33554432 | bytes 9175428 | tf_op jit(solution)/shard_map/convert
  310.4 2.3 fusion.54
  314.2 1.4 dynamic-slice_reduce_fusion.3
  316.1 35.8 %multiply_convert_fusion.7 = (bf16[32,65536]{1,0:T(8,128)(2,1)S(1)}, bf16[32,65536]{1,0:T(8,128)(2,1)S(1)}) fusion(f32[65536]{0:T(1024)S(1)} %get-tuple-element.290, f32[32]{0:T(128)S(1)} %get-tuple-element.291, f32[65536]{0:T(1024)S(1)} %get-tuple-element.288, f32[32]{0:T(128)S(1)} %get-tuple-element.289, f32[65536]{0:T(1024)S(1)} %get-tuple-element.286, ...), kind=kLoop, calls=%fused_computation.11.clone.1 | loop fusion | flops 33554432 | bytes 9175428 | tf_op jit(solution)/shard_map/convert
  351.9 2.3 fusion.54
  355.6 1.4 dynamic-slice_reduce_fusion.3
  357.5 35.8 %multiply_convert_fusion.7 = (bf16[32,65536]{1,0:T(8,128)(2,1)S(1)}, bf16[32,65536]{1,0:T(8,128)(2,1)S(1)}) fusion(f32[65536]{0:T(1024)S(1)} %get-tuple-element.290, f32[32]{0:T(128)S(1)} %get-tuple-element.291, f32[65536]{0:T(1024)S(1)} %get-tuple-element.288, f32[32]{0:T(128)S(1)} %get-tuple-element.289, f32[65536]{0:T(1024)S(1)} %get-tuple-element.286, ...), kind=kLoop, calls=%fused_computation.11.clone.1 | loop fusion | flops 33554432 | bytes 9175428 | tf_op jit(solution)/shard_map/convert
  393.3 2.3 fusion.54
  397.0 1.4 dynamic-slice_reduce_fusion.3
  398.9 35.8 %multiply_convert_fusion.7 = (bf16[32,65536]{1,0:T(8,128)(2,1)S(1)}, bf16[32,65536]{1,0:T(8,128)(2,1)S(1)}) fusion(f32[65536]{0:T(1024)S(1)} %get-tuple-element.290, f32[32]{0:T(128)S(1)} %get-tuple-element.291, f32[65536]{0:T(1024)S(1)} %get-tuple-element.288, f32[32]{0:T(128)S(1)} %get-tuple-element.289, f32[65536]{0:T(1024)S(1)} %get-tuple-element.286, ...), kind=kLoop, calls=%fused_computation.11.clone.1 | loop fusion | flops 33554432 | bytes 9175428 | tf_op jit(solution)/shard_map/convert
  434.7 2.3 fusion.54
  438.5 1.4 dynamic-slice_reduce_fusion.3
  440.4 35.8 %multiply_convert_fusion.7 = (bf16[32,65536]{1,0:T(8,128)(2,1)S(1)}, bf16[32,65536]{1,0:T(8,128)(2,1)S(1)}) fusion(f32[65536]{0:T(1024)S(1)} %get-tuple-element.290, f32[32]{0:T(128)S(1)} %get-tuple-element.291, f32[65536]{0:T(1024)S(1)} %get-tuple-element.288, f32[32]{0:T(128)S(1)} %get-tuple-element.289, f32[65536]{0:T(1024)S(1)} %get-tuple-element.286, ...), kind=kLoop, calls=%fused_computation.11.clone.1 | loop fusion | flops 33554432 | bytes 9175428 | tf_op jit(solution)/shard_map/convert
  476.2 2.3 fusion.54
  479.9 1.4 dynamic-slice_reduce_fusion.3
  481.8 35.8 %multiply_convert_fusion.7 = (bf16[32,65536]{1,0:T(8,128)(2,1)S(1)}, bf16[32,65536]{1,0:T(8,128)(2,1)S(1)}) fusion(f32[65536]{0:T(1024)S(1)} %get-tuple-element.290, f32[32]{0:T(128)S(1)} %get-tuple-element.291, f32[65536]{0:T(1024)S(1)} %get-tuple-element.288, f32[32]{0:T(128)S(1)} %get-tuple-element.289, f32[65536]{0:T(1024)S(1)} %get-tuple-element.286, ...), kind=kLoop, calls=%fused_computation.11.clone.1 | loop fusion | flops 33554432 | bytes 9175428 | tf_op jit(solution)/shard_map/convert
  517.6 2.3 fusion.54
  520.0 16.6 %all-gather = f32[32,4,2,32]{3,1,2,0:T(4,128)S(1)} all-gather(f32[8,4,2,32]{3,1,2,0:T(4,128)S(1)} %get-tuple-element.42), channel_id=2, replica_groups=mesh['grp'=4,'freq'=64] {'grp'}, dimensions={0}, use_global_device_ids=true | all-gather | bytes 40960 | tf_op jit(solution)/shard_map/all_gather | solution.py:14
  (89 shorter events, 58.1 us)
Async XLA Ops:
  87.2 37.2 %all-to-all-start = ((bf16[64,16,1024]{2,1,0:T(8,128)(2,1)}), bf16[64,16,1024]{2,1,0:T(8,128)(2,1)S(1)}, u32[]{:S(2)}, u32[]{:S(2)}) async-start(bf16[64,16,1024]{2,1,0:T(8,128)(2,1)} %constant_dynamic-update-slice_fusion), calls=%async_computation | async-start | bytes 4194304 | tf_op jit(solution)/shard_map/all_to_all | solution.py:65
  145.8 7.3 %copy-start.1 = (f32[3,65536]{1,0:T(4,128)S(1)}, f32[3,65536]{1,0:T(4,128)}, u32[]{:S(2)}) copy-start(f32[3,65536]{1,0:T(4,128)} %param.8) | copy-start | bytes 2359300
  145.8 8.7 %copy-start.4 = (f32[3,2048]{1,0:T(4,128)S(1)}, f32[3,2048]{1,0:T(4,128)}, u32[]{:S(2)}) copy-start(f32[3,2048]{1,0:T(4,128)} %param.10) | copy-start | bytes 73732
  145.8 35.2 %all-to-all-start.1 = ((bf16[64,16,1024]{2,1,0:T(8,128)(2,1)}), bf16[64,16,1024]{2,1,0:T(8,128)(2,1)S(1)}, u32[]{:S(2)}, u32[]{:S(2)}) async-start(bf16[64,16,1024]{2,1,0:T(8,128)(2,1)} %bitcast.154), calls=%async_computation.1 | async-start | bytes 4194304 | tf_op jit(solution)/shard_map/all_to_all | solution.py:70
  153.1 1.7 copy-start.5
  183.5 5.0 copy-start
  183.5 5.0 copy-start.2
  183.5 5.0 copy-start.3
